TPU v7x, 32 devices: a whole 2x2x4 slice. The times are simulated.
32 devices in a mesh: groups: 2 (over y), seq: 4 (over z), heads: 2 (over x), cfg: 2 (over core).
Axes of the slice: x: 2, y: 2, z: 4, core: 2. Of those that a mesh axis runs over, the one named last changes fastest.
Arguments:
- video_tokens: bfloat16 [2, 8, 1152, 1024], P('cfg', ('groups', 'seq'), 'heads'), parts along dimension 1, may hold values from -6 to 6
- text_tokens: bfloat16 [2, 8, 1152, 128], P('cfg', ('groups', 'seq'), 'heads'), parts along dimension 1, may hold values from -6 to 6
- text_length: int32 [2, 8], P('cfg', ('groups', 'seq')), parts along dimension 1, may hold values from 1 to 128
- guide_numer: int32 [8], P(('groups', 'seq')), parts along dimension 0, may hold values from 2 to 8
- guide_denom: int32 [8], P(('groups', 'seq')), parts along dimension 0, may hold values from 4 to 8
- spatial_gain: bfloat16 [1152], replicated, may hold values from 0.25 to 1.75
- spatial_qkv: bfloat16 [3, 1152, 1152], P(None, 'heads'), may hold values from -0.11785113 to 0.11785113
- spatial_out: bfloat16 [1152, 1152], P('heads'), may hold values from -0.1875 to 0.1875
- temporal_gain: bfloat16 [1152], replicated, may hold values from 0.25 to 1.75
- temporal_qkv: bfloat16 [3, 1152, 1152], P(None, 'heads'), may hold values from -0.11785113 to 0.11785113
- temporal_out: bfloat16 [1152, 1152], P('heads'), may hold values from -0.1875 to 0.1875
Outputs:
- guided: bfloat16 [8, 1152, 1024], P(('groups', 'seq'), ('heads', 'cfg')), parts along dimension 0
There are 2 independent parts, one for each index of `groups`. A program takes and returns all parts, laid end to end along the dimension named above; an argument that names none is the same for every part. Nothing has to cross between parts.
Inputs may be any that keep to these rules, and one draw needn't show every extreme that they name: `text_length`: text tokens at or beyond a frame's length are padding.
All inputs are finite; a program needn't handle non-finite values.
Results may differ from a plain program's by a relative error of at most 0.009.
Values may be sent and summed in bfloat16 or wider, within the bound.
A program may use at most 64 MiB of HBM per device.

v0:
```python
import jax
import jax.numpy as jnp
from jax import lax
from jax.sharding import PartitionSpec as P

D = 1152
HEAD_DIM = 72
epsilon = 1e-06


def from_partner(shard, axis, stride):
    return lax.ppermute(shard, axis, [(i, i ^ 1 << stride) for i in range(lax.axis_size(axis))])


def softmax_along(scores, axis):
    top_score = jnp.max(scores, axis=axis, keepdims=True)
    expons = jnp.exp(scores - top_score)
    return (expons / jnp.sum(expons, axis=axis, keepdims=True)).astype(jnp.bfloat16)


def project_piece(piece, gain_vector, weights, parts):
    gain_piece = gain_vector.astype(jnp.float32)
    weight_piece = weights[parts]
    piece_wide = piece.astype(jnp.float32)
    scaled = (piece_wide * gain_piece[None, :, None]).astype(jnp.bfloat16)
    product = jnp.einsum("kod,fdp->fkop", weight_piece, scaled, preferred_element_type=jnp.float32)
    return (product, jnp.sum(piece_wide * piece_wide, axis=1))


def add_mixed(piece, matrix):
    return jnp.einsum("oc,fcp->fop", matrix, piece, preferred_element_type=jnp.float32)


def shards(
    video_tokens,
    text_tokens,
    text_length,
    guide_numer,
    guide_denom,
    spatial_gain,
    spatial_qkv,
    spatial_out,
    temporal_gain,
    temporal_qkv,
    temporal_out,
):
    frame_count = video_tokens.shape[1]
    width = video_tokens.shape[2]
    positions = video_tokens.shape[3]
    text_count = text_tokens.shape[3]
    local_heads = width // HEAD_DIM
    frame_tokens = video_tokens[0]
    frame_text = text_tokens[0]
    video_piece = lax.all_gather(frame_tokens, "heads", axis=1, tiled=True)
    text_piece = lax.all_gather(frame_text, "heads", axis=1, tiled=True)
    video_add, video_sq = project_piece(video_piece, spatial_gain, spatial_qkv, slice(0, 3))
    text_add, text_sq = project_piece(text_piece, spatial_gain, spatial_qkv, slice(1, 3))
    mixed = (video_add * lax.rsqrt(video_sq / D + epsilon)[:, None, None, :]).astype(jnp.bfloat16)
    mixed = mixed.reshape(frame_count, 3, local_heads, HEAD_DIM, positions)
    context = (text_add * lax.rsqrt(text_sq / D + epsilon)[:, None, None, :]).astype(jnp.bfloat16)
    context = context.reshape(frame_count, 2, local_heads, HEAD_DIM, text_count)
    key_rows = jnp.concatenate([mixed[:, 1], context[:, 0]], axis=3)
    value_rows = jnp.concatenate([mixed[:, 2], context[:, 1]], axis=3)
    query_all = mixed[:, 0]
    text_valid = jnp.arange(text_count, dtype=jnp.int32)[None, :] < text_length[0][:, None]
    valid_keys = jnp.concatenate(
        [jnp.ones((frame_count, positions), dtype=bool), text_valid], axis=1
    )
    block_rows = min(512, positions)
    block_count = positions // block_rows
    frame_ids = jnp.repeat(jnp.arange(frame_count, dtype=jnp.int32), block_count)
    block_ids = jnp.tile(jnp.arange(block_count, dtype=jnp.int32), frame_count)

    def block_step(inputs):
        frame_id, block_id = inputs
        query_rows = lax.dynamic_slice_in_dim(
            query_all[frame_id], block_id * block_rows, block_rows, 2
        )
        scores = jnp.einsum(
            "hep,hek->hpk", query_rows, key_rows[frame_id], preferred_element_type=jnp.float32
        )
        scores = scores * HEAD_DIM ** (-0.5)
        scores = jnp.where(valid_keys[frame_id][None, None, :], scores, -jnp.inf)
        weights = softmax_along(scores, 2)
        result = jnp.einsum(
            "hpk,hek->hep", weights, value_rows[frame_id], preferred_element_type=jnp.float32
        )
        return result.astype(jnp.bfloat16)

    attended = lax.map(block_step, (frame_ids, block_ids))
    attended = attended.reshape(frame_count, block_count, local_heads, HEAD_DIM, block_rows)
    attended = jnp.transpose(attended, (0, 2, 3, 1, 4)).reshape(frame_count, width, positions)
    update = add_mixed(lax.all_gather(attended, "heads", axis=1, tiled=True), spatial_out)
    after_spatial = (frame_tokens.astype(jnp.float32) + update).astype(jnp.bfloat16)
    own_rows = lax.all_to_all(after_spatial, "seq", split_axis=2, concat_axis=0, tiled=True)
    frames_all = own_rows.shape[0]
    columns = own_rows.shape[2]
    piece_add, piece_sq = project_piece(
        lax.all_gather(own_rows, "heads", axis=1, tiled=True),
        temporal_gain,
        temporal_qkv,
        slice(0, 3),
    )
    mixed_time = (piece_add * lax.rsqrt(piece_sq / D + epsilon)[:, None, None, :]).astype(
        jnp.bfloat16
    )
    mixed_time = mixed_time.reshape(frames_all, 3, local_heads, HEAD_DIM, columns)
    time_scores = jnp.einsum(
        "fhep,ghep->hfgp", mixed_time[:, 0], mixed_time[:, 1], preferred_element_type=jnp.float32
    )
    time_weights = softmax_along(time_scores * HEAD_DIM ** (-0.5), 2)
    attended_time = jnp.einsum(
        "hfgp,ghep->fhep", time_weights, mixed_time[:, 2], preferred_element_type=jnp.float32
    )
    attended_time = attended_time.astype(jnp.bfloat16).reshape(frames_all, width, columns)
    update_time = add_mixed(
        lax.all_gather(attended_time, "heads", axis=1, tiled=True), temporal_out
    )
    block_out = (own_rows.astype(jnp.float32) + update_time).astype(jnp.bfloat16)
    returned = lax.all_to_all(block_out, "seq", split_axis=0, concat_axis=2, tiled=True)
    half_width = width // 2
    partner = from_partner(returned, "cfg", 0)
    branch_index = lax.axis_index("cfg")
    cond_full = jnp.where(branch_index == 0, returned, partner)
    uncond_full = jnp.where(branch_index == 0, partner, returned)
    cond_part = lax.dynamic_slice_in_dim(cond_full, branch_index * half_width, half_width, 1)
    uncond_part = lax.dynamic_slice_in_dim(uncond_full, branch_index * half_width, half_width, 1)
    ratio = guide_numer.astype(jnp.float32) / guide_denom.astype(jnp.float32)
    cond_wide = cond_part.astype(jnp.float32)
    uncond_wide = uncond_part.astype(jnp.float32)
    return (uncond_wide + ratio[:, None, None] * (cond_wide - uncond_wide)).astype(jnp.bfloat16)


def solution(mesh):
    return jax.shard_map(
        shards,
        mesh=mesh,
        in_specs=(
            P("cfg", ("groups", "seq"), "heads", None),
            P("cfg", ("groups", "seq"), "heads", None),
            P("cfg", ("groups", "seq")),
            P(("groups", "seq")),
            P(("groups", "seq")),
            P(),
            P(None, "heads", None),
            P("heads", None),
            P(),
            P(None, "heads", None),
            P("heads", None),
        ),
        out_specs=P(("groups", "seq"), ("heads", "cfg"), None),
        check_vma=False,
    )
```

profile of v0, /device:TPU:0, one launch (start us, length us, event | category | flops | bytes accessed | tf_op | source)
XLA Modules:
  0.0 359.0 jit_solution(843548291912899709)
XLA Ops:
  8.7 7.7 %all-gather.1 = bf16[1,1,1152,128]{3,2,1,0:T(8,128)(2,1)S(1)} all-gather(bf16[1,1,576,128]{3,2,1,0:T(8,128)(2,1)} %param.14), channel_id=3, replica_groups=mesh['groups'=2,'seq'=4,'heads'=2,'cfg'=2] {'heads'}, dimensions={2}, use_global_device_ids=true | all-gather | bytes 442368 | tf_op jit(solution)/shard_map/all_gather | solution.py:55
  16.6 3.0 fusion.87
  19.6 28.1 %all-gather.12.cloned.1.call-done = bf16[1,1,1152,1024]{3,2,1,0:T(8,128)(2,1)} async-done(((bf16[1,1,576,1024]{3,2,1,0:T(8,128)(2,1)}), bf16[1,1,1152,1024]{3,2,1,0:T(8,128)(2,1)}) %all-gather.12.cloned.1.call-update) | async-done | bytes 2359312 | tf_op jit(solution)/shard_map/all_gather | solution.py:54
  50.1 7.3 %fusion.48 = bf16[1,1024,3,576]{1,3,2,0:T(8,128)(2,1)S(1)} fusion(f32[1024]{0:T(1024)S(1)} %add_rsqrt_fusion.1, bf16[3,576,1152]{2,1,0:T(8,128)(2,1)} %param.19, bf16[1,1,1152,1024]{3,2,1,0:T(8,128)(2,1)S(1)} %copy-done.3, f32[1152]{0:T(1024)S(1)} %convert_element_type.98), kind=kOutput, calls=%fused_computation.28 | convolution fusion | flops 4083941376 | bytes 9888256 | tf_op jit(solution)/shard_map/kod,fdp->fkop/dot_general | solution.py:26
  60.1 37.0 %while.10 = (s32[]{:T(128)}, bf16[2,8,72,512]{3,2,1,0:T(8,128)(2,1)}, pred[1,1152]{1,0:T(4,128)(4,1)S(1)}, s32[2]{0:T(128)S(1)}, bf16[1,8,72,1024]{3,2,1,0:T(8,1...) while((s32[]{:T(128)}, ...), condition=%wide.region_5.6_spmd, body=%wide.region_2.5_spmd.sunk | while | flops 2081200384 | bytes 5788856 | solution.py:90
  61.9 7.0 %exponential_reduce_fusion.2 = f32[8,512]{1,0:T(8,128)S(1)} fusion(pred[1152]{0:T(1024)(128)(4,1)S(1)} %reduce.5, bf16[1,8,72,1152]{3,2,1,0:T(8,128)(2,1)S(1)} %get-tuple-element.139, bf16[1,8,72,1024]{3,2,1,0:T(8,128)(2,1)} %get-tuple-element.138, s32[]{:T(128)S(6)} %select_n.52), kind=kOutput, calls=%fused_computation.5.clone.1 | convolution fusion | flops 698352768 | bytes 1934468 | tf_op jit(solution)/shard_map/while/body/eval_jaxpr/sub | solution.py:17
  69.0 9.8 %fusion.120 = bf16[2,8,72,512]{3,2,1,0:T(8,128)(2,1)} fusion(bf16[2,8,72,512]{3,2,1,0:T(8,128)(2,1)} %get-tuple-element.123, s32[]{:T(128)} %get-tuple-element.122, bf16[1,8,72,1152]{3,2,1,0:T(8,128)(2,1)} %get-tuple-element.140, f32[8,512]{1,0:T(8,128)S(1)} %exponential_reduce_fusion.2, pred[1152]{0:T(1024)(128)(4,1)S(1)} %reduce.5, ...), kind=kOutput, calls=%fused_computation.13.clone.1 | convolution fusion | flops 1382847616 | bytes 3851908 | tf_op jit(solution)/shard_map/while/body/eval_jaxpr/hpk,hek->hep/dot_general | solution.py:85
  80.2 7.0 %exponential_reduce_fusion.2 = f32[8,512]{1,0:T(8,128)S(1)} fusion(pred[1152]{0:T(1024)(128)(4,1)S(1)} %reduce.5, bf16[1,8,72,1152]{3,2,1,0:T(8,128)(2,1)S(1)} %get-tuple-element.139, bf16[1,8,72,1024]{3,2,1,0:T(8,128)(2,1)} %get-tuple-element.138, s32[]{:T(128)S(6)} %select_n.52), kind=kOutput, calls=%fused_computation.5.clone.1 | convolution fusion | flops 698352768 | bytes 1934468 | tf_op jit(solution)/shard_map/while/body/eval_jaxpr/sub | solution.py:17
  87.2 9.8 %fusion.120 = bf16[2,8,72,512]{3,2,1,0:T(8,128)(2,1)} fusion(bf16[2,8,72,512]{3,2,1,0:T(8,128)(2,1)} %get-tuple-element.123, s32[]{:T(128)} %get-tuple-element.122, bf16[1,8,72,1152]{3,2,1,0:T(8,128)(2,1)} %get-tuple-element.140, f32[8,512]{1,0:T(8,128)S(1)} %exponential_reduce_fusion.2, pred[1152]{0:T(1024)(128)(4,1)S(1)} %reduce.5, ...), kind=kOutput, calls=%fused_computation.13.clone.1 | convolution fusion | flops 1382847616 | bytes 3851908 | tf_op jit(solution)/shard_map/while/body/eval_jaxpr/hpk,hek->hep/dot_general | solution.py:85
  101.5 36.0 %all-gather.8.cloned.1.call-done = bf16[1,1152,1024]{2,1,0:T(8,128)(2,1)} async-done(((bf16[1,576,1024]{2,1,0:T(8,128)(2,1)}), bf16[1,1152,1024]{2,1,0:T(8,128)(2,1)}) %all-gather.8.cloned.1.call-update) | async-done | bytes 2359312 | tf_op jit(solution)/shard_map/all_gather | solution.py:93
  137.5 3.7 %fusion.64 = bf16[1,576,1024]{2,1,0:T(8,128)(2,1)S(1)} fusion(bf16[576,1152]{1,0:T(8,128)(2,1)S(1)} %copy-done, bf16[1,1152,1024]{2,1,0:T(8,128)(2,1)} %all-gather.8.cloned.1.call-done, bf16[1,1,576,1024]{3,2,1,0:T(8,128)(2,1)} %param.13), kind=kOutput, calls=%fused_computation.47 | convolution fusion | flops 1360723968 | bytes 6045696 | tf_op jit(solution)/shard_map/oc,fcp->fop/dot_general | solution.py:31
  141.1 4.1 %copy.44 = bf16[1,576,1024]{1,0,2:T(2,128)(2,1)} copy(bf16[1,576,1024]{2,1,0:T(8,128)(2,1)S(1)} %fusion.64) | data formatting | bytes 2359296 | tf_op jit(solution)/shard_map/convert_element_type | solution.py:94
  145.8 9.9 %reduce.3 = bf16[1024,576]{1,0:T(8,128)(2,1)S(1)} reduce(bf16[1024,1,576]{2,1,0:T(2,128)(2,1)} %bitcast.189, bf16[]{:T(256)} %broadcast.82), dimensions={1}, to_apply=%bitcast.164.reduce_sub_computation | reduce | bytes 2359298
  158.3 33.0 %all_to_all.36 = bf16[4,2,73728]{2,1,0:T(2,128)(2,1)S(1)} all-to-all(bf16[4,2,73728]{2,1,0:T(2,128)(2,1)} %reshape.124), channel_id=1, replica_groups=mesh['groups'=2,'seq'=4,'heads'=2,'cfg'=2] {'seq'}, dimensions={0} | all-to-all | bytes 2359296 | tf_op jit(solution)/shard_map/all_to_all | solution.py:95
  191.3 3.3 reshape.125
  198.3 34.1 %all-gather.14.cloned.1.call-done = bf16[4,1,1152,256]{3,2,0,1:T(8,128)(2,1)} async-done(((bf16[4,1,576,256]{3,2,0,1:T(8,128)(2,1)}), bf16[4,1,1152,256]{3,2,0,1:T(8,128)(2,1)}) %all-gather.14.cloned.1.call-update) | async-done | bytes 2359312 | tf_op jit(solution)/shard_map/all_gather | solution.py:99
  234.7 7.2 %multiply_convert_fusion = bf16[4,256,3,576]{1,3,2,0:T(8,128)(2,1)S(1)} fusion(f32[4,256]{1,0:T(4,128)S(1)} %add_rsqrt_fusion, bf16[3,576,1152]{2,1,0:T(8,128)(2,1)} %param.22, bf16[4,1,1152,256]{3,2,0,1:T(8,128)(2,1)S(1)} %copy-done.4, f32[1152]{0:T(1024)S(1)} %convert_element_type.109), kind=kOutput, calls=%fused_computation.29 | convolution fusion | flops 4083941376 | bytes 9888256 | tf_op jit(solution)/shard_map/kod,fdp->fkop/dot_general | solution.py:26
  246.7 4.1 %copy.60 = bf16[4,1,8,72,256]{3,0,4,2,1:T(4,128)(2,1)} copy(bf16[4,1,8,72,256]{4,3,2,1,0:T(8,128)(2,1)} %get-tuple-element.59) | data formatting | bytes 2359296
  250.7 5.8 %fusion.71 = f32[8,256,4,4]{3,2,1,0:T(4,128)} fusion(bf16[4,1,8,72,256]{3,0,4,2,1:T(4,128)(2,1)} %copy.60, bf16[4,1,8,72,256]{3,0,4,2,1:T(4,128)(2,1)S(1)} %copy.59), kind=kOutput, calls=%fused_computation.54 | convolution fusion | flops 4718592 | bytes 2490368 | tf_op jit(solution)/shard_map/fhep,ghep->hfgp/dot_general | solution.py:108
  264.1 5.8 %convert_bitcast_fusion = bf16[4,8,72,256]{2,0,3,1:T(4,128)(2,1)} fusion(bf16[8,4,4,256]{2,1,3,0:T(4,128)(2,1)} %copy.51, bf16[4,1,8,72,256]{3,0,4,2,1:T(4,128)(2,1)} %copy.58), kind=kOutput, calls=%fused_computation.59 | convolution fusion | flops 5308416 | bytes 2424832 | tf_op jit(solution)/shard_map/hfgp,ghep->fhep/dot_general | solution.py:112
  269.9 4.2 %copy.52 = bf16[4,8,72,256]{3,2,1,0:T(8,128)(2,1)} copy(bf16[4,8,72,256]{2,0,3,1:T(4,128)(2,1)} %convert_bitcast_fusion) | data formatting | bytes 2359296 | tf_op jit(solution)/shard_map/convert_element_type | solution.py:115
  274.1 36.2 %all-gather.10.cloned.1.call-done = bf16[4,1152,256]{2,1,0:T(8,128)(2,1)} async-done(((bf16[4,576,256]{2,1,0:T(8,128)(2,1)}), bf16[4,1152,256]{2,1,0:T(8,128)(2,1)}) %all-gather.10.cloned.1.call-update) | async-done | bytes 2359312 | tf_op jit(solution)/shard_map/all_gather | solution.py:117
  310.3 3.8 %fusion.63 = bf16[4,576,256]{2,1,0:T(8,128)(2,1)S(1)} fusion(bf16[4,1152,256]{2,1,0:T(8,128)(2,1)} %all-gather.10.cloned.1.call-done, bf16[576,1152]{1,0:T(8,128)(2,1)} %param.23, bf16[1,576,4,256]{3,1,2,0:T(8,128)(2,1)S(1)} %copy-done.2), kind=kOutput, calls=%fused_computation.45 | convolution fusion | flops 1360723968 | bytes 6045696 | tf_op jit(solution)/shard_map/oc,fcp->fop/dot_general | solution.py:31
  314.1 32.8 %all_to_all.37 = bf16[4,576,256]{2,1,0:T(8,128)(2,1)S(1)} all-to-all(bf16[4,576,256]{2,1,0:T(8,128)(2,1)S(1)} %fusion.63), channel_id=1, replica_groups=mesh['groups'=2,'seq'=4,'heads'=2,'cfg'=2] {'seq'}, dimensions={0} | all-to-all | bytes 2359296 | tf_op jit(solution)/shard_map/all_to_all | solution.py:120
  (57 shorter events, 38.0 us)
Async XLA Ops:
  6.5 130.9 %copy-start = (bf16[576,1152]{1,0:T(8,128)(2,1)S(1)}, bf16[576,1152]{1,0:T(8,128)(2,1)}, u32[]{:S(2)}) copy-start(bf16[576,1152]{1,0:T(8,128)(2,1)} %param.20) | copy-start | bytes 3981316
  6.5 41.1 %all-gather.12.cloned.1.call-start = ((), (), s32[]{:S(2)}) async-start(), calls=%async_computation.4 | async-start | bytes 3538944 | tf_op jit(solution)/shard_map/all_gather | solution.py:54
  7.3 130.2 %all-gather.8.cloned.1.call-start = ((), (), s32[]{:S(2)}) async-start(), calls=%async_computation.2 | async-start | bytes 3538944 | tf_op jit(solution)/shard_map/all_gather | solution.py:93
  47.7 2.4 copy-start.3
  101.3 131.0 %all-gather.14.cloned.1.call-start = ((), (), s32[]{:S(2)}) async-start(), calls=%async_computation.5 | async-start | bytes 3538944 | tf_op jit(solution)/shard_map/all_gather | solution.py:99
  196.5 1.8 copy-start.5
  198.0 112.3 %all-gather.10.cloned.1.call-start = ((), (), s32[]{:S(2)}) async-start(), calls=%async_computation.3 | async-start | bytes 3538944 | tf_op jit(solution)/shard_map/all_gather | solution.py:117
  232.3 2.4 copy-start.4
  259.4 2.2 copy-start.1
  269.9 40.4 %copy-start.2 = (bf16[1,576,4,256]{3,1,2,0:T(8,128)(2,1)S(1)}, bf16[1,576,4,256]{3,1,2,0:T(8,128)(2,1)}, u32[]{:S(2)}) copy-start(bf16[1,576,4,256]{3,1,2,0:T(8,128)(2,1)} %copy.46) | copy-start | bytes 3538948
  347.0 3.0 collective-permute-start
Sparse Core Ops, SparseCore 0:
  8.9 38.7 all-gather.11
  101.4 36.0 all-gather.7
  198.1 34.1 all-gather.13
  274.2 36.0 all-gather.9
where the time goes:
time: 364 us; the launch traced here: 359 us
  waiting for transfers between devices  137 us (38%)
  blocking collectives  73.5 us (20%)
  matrix products  70.3 us (19%)
  local copies, waits for them, and re-layouts  41.4 us (11%)
  other arithmetic  19.1 us (5%)
  between operations  15.5 us (4%)
    all_gather x1, waiting for transfers between devices, shards(): lax.all_gather(attended_time, 'heads', axis=1, tiled=True)  36.2 us
    all_gather x1, waiting for transfers between devices, shards(): lax.all_gather(attended, 'heads', axis=1, tiled=True)  36 us
    all_gather x1, waiting for transfers between devices, shards(): lax.all_gather(own_rows, 'heads', axis=1, tiled=True)  34.1 us
    all_to_all x1, blocking collectives, shards(): lax.all_to_all(after_spatial, 'seq', split_axis=2, concat_axis=0, tiled=T...  33 us
    all_to_all x1, blocking collectives, shards(): lax.all_to_all(block_out, 'seq', split_axis=0, concat_axis=2, tiled=True)  32.8 us
    all_gather x1, waiting for transfers between devices, shards(): video_piece = lax.all_gather(frame_tokens, 'heads', axis=1, tiled=True)  28.1 us
    dot_general x2, matrix products, block_step(): jnp.einsum('hpk,hek->hep', weights, value_rows[frame_id], preferred_eleme...  19.7 us
    unnamed x19, local copies, waits for them, and re-layouts  17.8 us
  transfers between devices with their start and end apart: 5, of which 5 were waited for; matrix products, arithmetic and copies ran while one was open for 1% of the time, Pallas kernels for 0%

commit v1 on v0

--- a/solution.py
+++ b/solution.py
@@ -6,6 +6,30 @@
 D = 1152
 HEAD_DIM = 72
 epsilon = 1e-06
+
+
+def cut_along(array, dim, size):
+    shape = array.shape
+    blocks = array.reshape(*shape[:dim], size, shape[dim] // size, *shape[dim + 1 :])
+    return jnp.moveaxis(blocks, dim, 0)
+
+
+def in_order(blocks, dim):
+    blocks = jnp.moveaxis(blocks, 0, dim)
+    shape = blocks.shape
+    return blocks.reshape(*shape[:dim], shape[dim] * shape[dim + 1], *shape[dim + 2 :])
+
+
+def rotated_exchange(x, axis, split_dim, concat_dim):
+    count, index = (lax.axis_size(axis), lax.axis_index(axis))
+    blocks = cut_along(x, split_dim, count)
+    whole = blocks
+    for hop in range(1, count):
+        target, source = ((index + hop) % count, (index - hop) % count)
+        sent = lax.dynamic_index_in_dim(blocks, target, 0)
+        other = lax.ppermute(sent, axis, [(i, (i + hop) % count) for i in range(count)])
+        whole = lax.dynamic_update_slice_in_dim(whole, other, source, axis=0)
+    return in_order(whole, concat_dim)
 
 
 def from_partner(shard, axis, stride):
@@ -117,7 +141,7 @@
         lax.all_gather(attended_time, "heads", axis=1, tiled=True), temporal_out
     )
     block_out = (own_rows.astype(jnp.float32) + update_time).astype(jnp.bfloat16)
-    returned = lax.all_to_all(block_out, "seq", split_axis=0, concat_axis=2, tiled=True)
+    returned = rotated_exchange(block_out, "seq", 0, 2)
     half_width = width // 2
     partner = from_partner(returned, "cfg", 0)
     branch_index = lax.axis_index("cfg")

time: 364 us -> 361 us (level)
  the two profiles are of different devices: /device:TPU:0 before, /device:TPU:9 now
where the time goes in v1:
time: 361 us; the launch traced here: 357 us
  waiting for transfers between devices  163 us (45%)
  matrix products  70.1 us (19%)
  local copies, waits for them, and re-layouts  45.9 us (13%)
  blocking collectives  35.9 us (10%)
  other arithmetic  19.1 us (5%)
  between operations  15.6 us (4%)
  starting transfers between devices  4.71 us (1%)
    all_gather x1, waiting for transfers between devices, shards(): lax.all_gather(own_rows, 'heads', axis=1, tiled=True)  36.8 us
    all_gather x1, waiting for transfers between devices, shards(): lax.all_gather(attended_time, 'heads', axis=1, tiled=True)  36.2 us
    all_gather x1, waiting for transfers between devices, shards(): lax.all_gather(attended, 'heads', axis=1, tiled=True)  36 us
    all_to_all x1, blocking collectives, shards(): lax.all_to_all(after_spatial, 'seq', split_axis=2, concat_axis=0, tiled=T...  30.3 us
    all_gather x1, waiting for transfers between devices, shards(): video_piece = lax.all_gather(frame_tokens, 'heads', axis=1, tiled=True)  28.7 us
    ppermute x3, waiting for transfers between devices, rotated_exchange(): lax.ppermute(sent, axis, [(i, (i + hop) % count) for i in range(count)])  23.8 us
    dot_general x2, matrix products, block_step(): jnp.einsum('hpk,hek->hep', weights, value_rows[frame_id], preferred_eleme...  19.7 us
    unnamed x21, local copies, waits for them, and re-layouts  18.8 us
  transfers between devices with their start and end apart: 8, of which 8 were waited for; matrix products, arithmetic and copies ran while one was open for 1% of the time, Pallas kernels for 0%

profile of v1, /device:TPU:9, one launch (start us, length us, event | category | flops | bytes accessed | tf_op | source)
XLA Modules:
  0.0 356.5 jit_solution(16234193628592837940)
XLA Ops:
  8.7 5.6 %all-gather.1 = bf16[1,1,1152,128]{3,2,1,0:T(8,128)(2,1)S(1)} all-gather(bf16[1,1,576,128]{3,2,1,0:T(8,128)(2,1)} %param.14), channel_id=3, replica_groups=mesh['groups'=2,'seq'=4,'heads'=2,'cfg'=2] {'heads'}, dimensions={2}, use_global_device_ids=true | all-gather | bytes 442368 | tf_op jit(solution)/shard_map/all_gather | solution.py:79
  17.2 28.7 %all-gather.12.cloned.1.call-done = bf16[1,1,1152,1024]{3,2,1,0:T(8,128)(2,1)} async-done(((bf16[1,1,576,1024]{3,2,1,0:T(8,128)(2,1)}), bf16[1,1,1152,1024]{3,2,1,0:T(8,128)(2,1)}) %all-gather.12.cloned.1.call-update) | async-done | bytes 2359312 | tf_op jit(solution)/shard_map/all_gather | solution.py:78
  48.3 7.3 %fusion.48 = bf16[1,1024,3,576]{1,3,2,0:T(8,128)(2,1)S(1)} fusion(f32[1024]{0:T(1024)S(1)} %add_rsqrt_fusion.1, bf16[3,576,1152]{2,1,0:T(8,128)(2,1)} %param.19, bf16[1,1,1152,1024]{3,2,1,0:T(8,128)(2,1)S(1)} %copy-done.4, f32[1152]{0:T(1024)S(1)} %convert_element_type.98), kind=kOutput, calls=%fused_computation.28 | convolution fusion | flops 4083941376 | bytes 9888256 | tf_op jit(solution)/shard_map/kod,fdp->fkop/dot_general | solution.py:50
  58.3 37.0 %while.10 = (s32[]{:T(128)}, bf16[2,8,72,512]{3,2,1,0:T(8,128)(2,1)}, pred[1,1152]{1,0:T(4,128)(4,1)S(1)}, s32[2]{0:T(128)S(1)}, bf16[1,8,72,1024]{3,2,1,0:T(8,1...) while((s32[]{:T(128)}, ...), condition=%wide.region_5.6_spmd, body=%wide.region_2.5_spmd.sunk | while | flops 2081200384 | bytes 5788856 | solution.py:114
  60.2 7.0 %exponential_reduce_fusion.2 = f32[8,512]{1,0:T(8,128)S(1)} fusion(pred[1152]{0:T(1024)(128)(4,1)S(1)} %reduce.5, bf16[1,8,72,1152]{3,2,1,0:T(8,128)(2,1)S(1)} %get-tuple-element.142, bf16[1,8,72,1024]{3,2,1,0:T(8,128)(2,1)} %get-tuple-element.141, s32[]{:T(128)S(6)} %select_n.110), kind=kOutput, calls=%fused_computation.5.clone.1 | convolution fusion | flops 698352768 | bytes 1934468 | tf_op jit(solution)/shard_map/while/body/eval_jaxpr/sub | solution.py:41
  67.2 9.8 %fusion.120 = bf16[2,8,72,512]{3,2,1,0:T(8,128)(2,1)} fusion(bf16[2,8,72,512]{3,2,1,0:T(8,128)(2,1)} %get-tuple-element.126, s32[]{:T(128)} %get-tuple-element.125, bf16[1,8,72,1152]{3,2,1,0:T(8,128)(2,1)} %get-tuple-element.143, f32[8,512]{1,0:T(8,128)S(1)} %exponential_reduce_fusion.2, pred[1152]{0:T(1024)(128)(4,1)S(1)} %reduce.5, ...), kind=kOutput, calls=%fused_computation.13.clone.1 | convolution fusion | flops 1382847616 | bytes 3851908 | tf_op jit(solution)/shard_map/while/body/eval_jaxpr/hpk,hek->hep/dot_general | solution.py:109
  78.5 7.0 %exponential_reduce_fusion.2 = f32[8,512]{1,0:T(8,128)S(1)} fusion(pred[1152]{0:T(1024)(128)(4,1)S(1)} %reduce.5, bf16[1,8,72,1152]{3,2,1,0:T(8,128)(2,1)S(1)} %get-tuple-element.142, bf16[1,8,72,1024]{3,2,1,0:T(8,128)(2,1)} %get-tuple-element.141, s32[]{:T(128)S(6)} %select_n.110), kind=kOutput, calls=%fused_computation.5.clone.1 | convolution fusion | flops 698352768 | bytes 1934468 | tf_op jit(solution)/shard_map/while/body/eval_jaxpr/sub | solution.py:41
  85.5 9.8 %fusion.120 = bf16[2,8,72,512]{3,2,1,0:T(8,128)(2,1)} fusion(bf16[2,8,72,512]{3,2,1,0:T(8,128)(2,1)} %get-tuple-element.126, s32[]{:T(128)} %get-tuple-element.125, bf16[1,8,72,1152]{3,2,1,0:T(8,128)(2,1)} %get-tuple-element.143, f32[8,512]{1,0:T(8,128)S(1)} %exponential_reduce_fusion.2, pred[1152]{0:T(1024)(128)(4,1)S(1)} %reduce.5, ...), kind=kOutput, calls=%fused_computation.13.clone.1 | convolution fusion | flops 1382847616 | bytes 3851908 | tf_op jit(solution)/shard_map/while/body/eval_jaxpr/hpk,hek->hep/dot_general | solution.py:109
  99.8 36.0 %all-gather.8.cloned.1.call-done = bf16[1,1152,1024]{2,1,0:T(8,128)(2,1)} async-done(((bf16[1,576,1024]{2,1,0:T(8,128)(2,1)}), bf16[1,1152,1024]{2,1,0:T(8,128)(2,1)}) %all-gather.8.cloned.1.call-update) | async-done | bytes 2359312 | tf_op jit(solution)/shard_map/all_gather | solution.py:117
  135.7 3.7 %fusion.64 = bf16[1,576,1024]{2,1,0:T(8,128)(2,1)S(1)} fusion(bf16[576,1152]{1,0:T(8,128)(2,1)S(1)} %copy-done, bf16[1,1152,1024]{2,1,0:T(8,128)(2,1)} %all-gather.8.cloned.1.call-done, bf16[1,1,576,1024]{3,2,1,0:T(8,128)(2,1)} %param.13), kind=kOutput, calls=%fused_computation.47 | convolution fusion | flops 1360723968 | bytes 6045696 | tf_op jit(solution)/shard_map/oc,fcp->fop/dot_general | solution.py:55
  139.4 4.1 %copy.44 = bf16[1,576,1024]{1,0,2:T(2,128)(2,1)} copy(bf16[1,576,1024]{2,1,0:T(8,128)(2,1)S(1)} %fusion.64) | data formatting | bytes 2359296 | tf_op jit(solution)/shard_map/convert_element_type | solution.py:118
  144.0 9.9 %reduce.3 = bf16[1024,576]{1,0:T(8,128)(2,1)S(1)} reduce(bf16[1024,1,576]{2,1,0:T(2,128)(2,1)} %bitcast.194, bf16[]{:T(256)} %broadcast.88), dimensions={1}, to_apply=%bitcast.169.reduce_sub_computation | reduce | bytes 2359298
  156.6 30.3 %all_to_all.18 = bf16[4,2,73728]{2,1,0:T(2,128)(2,1)S(1)} all-to-all(bf16[4,2,73728]{2,1,0:T(2,128)(2,1)} %reshape.135), channel_id=1, replica_groups=mesh['groups'=2,'seq'=4,'heads'=2,'cfg'=2] {'seq'}, dimensions={0} | all-to-all | bytes 2359296 | tf_op jit(solution)/shard_map/all_to_all | solution.py:119
  186.8 3.3 reshape.136
  193.8 36.8 %all-gather.14.cloned.1.call-done = bf16[4,1,1152,256]{3,2,0,1:T(8,128)(2,1)} async-done(((bf16[4,1,576,256]{3,2,0,1:T(8,128)(2,1)}), bf16[4,1,1152,256]{3,2,0,1:T(8,128)(2,1)}) %all-gather.14.cloned.1.call-update) | async-done | bytes 2359312 | tf_op jit(solution)/shard_map/all_gather | solution.py:123
  232.9 7.2 %multiply_convert_fusion = bf16[4,256,3,576]{1,3,2,0:T(8,128)(2,1)S(1)} fusion(f32[4,256]{1,0:T(4,128)S(1)} %add_rsqrt_fusion, bf16[3,576,1152]{2,1,0:T(8,128)(2,1)} %param.22, bf16[4,1,1152,256]{3,2,0,1:T(8,128)(2,1)S(1)} %copy-done.5, f32[1152]{0:T(1024)S(1)} %convert_element_type.109), kind=kOutput, calls=%fused_computation.29 | convolution fusion | flops 4083941376 | bytes 9888256 | tf_op jit(solution)/shard_map/kod,fdp->fkop/dot_general | solution.py:50
  244.9 4.1 %copy.60 = bf16[4,1,8,72,256]{3,0,4,2,1:T(4,128)(2,1)} copy(bf16[4,1,8,72,256]{4,3,2,1,0:T(8,128)(2,1)} %get-tuple-element.59) | data formatting | bytes 2359296
  249.0 5.8 %fusion.71 = f32[8,256,4,4]{3,2,1,0:T(4,128)} fusion(bf16[4,1,8,72,256]{3,0,4,2,1:T(4,128)(2,1)} %copy.60, bf16[4,1,8,72,256]{3,0,4,2,1:T(4,128)(2,1)S(1)} %copy.59), kind=kOutput, calls=%fused_computation.54 | convolution fusion | flops 4718592 | bytes 2490368 | tf_op jit(solution)/shard_map/fhep,ghep->hfgp/dot_general | solution.py:132
  262.3 5.8 %convert_bitcast_fusion = bf16[4,8,72,256]{2,0,3,1:T(4,128)(2,1)} fusion(bf16[8,4,4,256]{2,1,3,0:T(4,128)(2,1)} %copy.51, bf16[4,1,8,72,256]{3,0,4,2,1:T(4,128)(2,1)} %copy.58), kind=kOutput, calls=%fused_computation.59 | convolution fusion | flops 5308416 | bytes 2424832 | tf_op jit(solution)/shard_map/hfgp,ghep->fhep/dot_general | solution.py:136
  268.2 4.2 %copy.52 = bf16[4,8,72,256]{3,2,1,0:T(8,128)(2,1)} copy(bf16[4,8,72,256]{2,0,3,1:T(4,128)(2,1)} %convert_bitcast_fusion) | data formatting | bytes 2359296 | tf_op jit(solution)/shard_map/convert_element_type | solution.py:139
  272.4 36.2 %all-gather.10.cloned.1.call-done = bf16[4,1152,256]{2,1,0:T(8,128)(2,1)} async-done(((bf16[4,576,256]{2,1,0:T(8,128)(2,1)}), bf16[4,1152,256]{2,1,0:T(8,128)(2,1)}) %all-gather.10.cloned.1.call-update) | async-done | bytes 2359312 | tf_op jit(solution)/shard_map/all_gather | solution.py:141
  308.6 3.8 %fusion.63 = bf16[4,576,256]{2,1,0:T(8,128)(2,1)S(1)} fusion(bf16[4,1152,256]{2,1,0:T(8,128)(2,1)} %all-gather.10.cloned.1.call-done, bf16[576,1152]{1,0:T(8,128)(2,1)} %param.23, bf16[1,576,4,256]{3,1,2,0:T(8,128)(2,1)S(1)} %copy-done.2), kind=kOutput, calls=%fused_computation.45 | convolution fusion | flops 1360723968 | bytes 6045696 | tf_op jit(solution)/shard_map/oc,fcp->fop/dot_general | solution.py:55
  317.1 4.1 %collective-permute-done = bf16[1,1,576,256]{3,2,0,1:T(8,128)(2,1)S(1)} collective-permute-done((bf16[1,1,576,256]{3,2,0,1:T(8,128)(2,1)S(1)}, bf16[1,1,576,256]{3,2,0,1:T(8,128)(2,1)S(1)}, u32[]{:S(2)}, u32[]{:S(2)}) %collective-permute-start) | collective-permute-done | bytes 294944 | tf_op jit(solution)/shard_map/ppermute | solution.py:30
  321.9 17.2 %collective-permute-done.1 = bf16[1,1,576,256]{3,2,0,1:T(8,128)(2,1)S(1)} collective-permute-done((bf16[1,1,576,256]{3,2,0,1:T(8,128)(2,1)S(1)}, bf16[1,1,576,256]{3,2,0,1:T(8,128)(2,1)S(1)}, u32[]{:S(2)}, u32[]{:S(2)}) %collective-permute-start.1) | collective-permute-done | bytes 294944 | tf_op jit(solution)/shard_map/ppermute | solution.py:30
  (68 shorter events, 51.3 us)
Async XLA Ops:
  6.5 129.2 %copy-start = (bf16[576,1152]{1,0:T(8,128)(2,1)S(1)}, bf16[576,1152]{1,0:T(8,128)(2,1)}, u32[]{:S(2)}) copy-start(bf16[576,1152]{1,0:T(8,128)(2,1)} %param.20) | copy-start | bytes 3981316
  6.5 39.4 %all-gather.12.cloned.1.call-start = ((), (), s32[]{:S(2)}) async-start(), calls=%async_computation.3 | async-start | bytes 3538944 | tf_op jit(solution)/shard_map/all_gather | solution.py:78
  7.3 128.5 %all-gather.8.cloned.1.call-start = ((), (), s32[]{:S(2)}) async-start(), calls=%async_computation.1 | async-start | bytes 3538944 | tf_op jit(solution)/shard_map/all_gather | solution.py:117
  45.9 2.4 copy-start.4
  99.5 131.0 %all-gather.14.cloned.1.call-start = ((), (), s32[]{:S(2)}) async-start(), calls=%async_computation.4 | async-start | bytes 3538944 | tf_op jit(solution)/shard_map/all_gather | solution.py:123
  192.0 1.8 copy-start.6
  193.5 115.0 %all-gather.10.cloned.1.call-start = ((), (), s32[]{:S(2)}) async-start(), calls=%async_computation.2 | async-start | bytes 3538944 | tf_op jit(solution)/shard_map/all_gather | solution.py:141
  230.6 2.4 copy-start.5
  257.7 2.2 copy-start.1
  268.2 40.4 %copy-start.2 = (bf16[1,576,4,256]{3,1,2,0:T(8,128)(2,1)S(1)}, bf16[1,576,4,256]{3,1,2,0:T(8,128)(2,1)}, u32[]{:S(2)}) copy-start(bf16[1,576,4,256]{3,1,2,0:T(8,128)(2,1)} %copy.46) | copy-start | bytes 3538948
  312.3 1.0 copy-start.3
  313.4 7.8 %collective-permute-start = (bf16[1,1,576,256]{3,2,0,1:T(8,128)(2,1)S(1)}, bf16[1,1,576,256]{3,2,0,1:T(8,128)(2,1)S(1)}, u32[]{:S(2)}, u32[]{:S(2)}) collective-permute-start(bf16[1,1,576,256]{3,2,0,1:T(8,128)(2,1)S(1)} %get-tuple-element.65), channel_id=1, source_target_pairs={{0,4},{4,8},{8,12},{12,0},{1,5},{5,9},{9,13},{13,1},{2,6},{6,10},{... | collective-permute-start | bytes 884744 | tf_op jit(solution)/shard_map/ppermute | solution.py:30
  314.7 24.5 %collective-permute-start.1 = (bf16[1,1,576,256]{3,2,0,1:T(8,128)(2,1)S(1)}, bf16[1,1,576,256]{3,2,0,1:T(8,128)(2,1)S(1)}, u32[]{:S(2)}, u32[]{:S(2)}) collective-permute-start(bf16[1,1,576,256]{3,2,0,1:T(8,128)(2,1)S(1)} %get-tuple-element.64), channel_id=1, source_target_pairs={{0,8},{4,12},{8,0},{12,4},{1,9},{5,13},{9,1},{13,5},{2,10},{6,14},... | collective-permute-start | bytes 884744 | tf_op jit(solution)/shard_map/ppermute | solution.py:30
  315.8 26.5 %collective-permute-start.2 = (bf16[1,1,576,256]{3,2,0,1:T(8,128)(2,1)S(1)}, bf16[1,1,576,256]{3,2,0,1:T(8,128)(2,1)S(1)}, u32[]{:S(2)}, u32[]{:S(2)}) collective-permute-start(bf16[1,1,576,256]{3,2,0,1:T(8,128)(2,1)S(1)} %get-tuple-element.63), channel_id=1, source_target_pairs={{0,12},{4,0},{8,4},{12,8},{1,13},{5,1},{9,5},{13,9},{2,14},{6,2},{... | collective-permute-start | bytes 884744 | tf_op jit(solution)/shard_map/ppermute | solution.py:30
  344.4 3.2 collective-permute-start.3
Sparse Core Ops, SparseCore 0:
  8.9 37.0 all-gather.11
  99.7 36.0 all-gather.7
  193.6 36.8 all-gather.13
  272.5 36.0 all-gather.9
